TPU v7x, 32 devices: a whole 2x2x4 slice. The times are simulated.
32 devices in a mesh: frag: 2 (over x), dev: 16 (over z, y, core).
Axes of the slice: x: 2, y: 2, z: 4, core: 2. Of those that a mesh axis runs over, the one named last changes fastest.
Arguments:
- ao_ints: bfloat16 [192, 96, 96, 96], P(('frag', 'dev')), parts along dimension 0
- coeffs: bfloat16 [192, 96], P('frag'), parts along dimension 0
Outputs:
- output: float32 [192, 96, 9216], P('frag', None, 'dev'), parts along dimension 0
There are 2 independent parts. A program takes and returns all parts, laid end to end along the dimension named above; each array names one.
All inputs are finite; a program needn't handle non-finite values.
Results may differ from a plain program's by a relative error of at most 0.001.
Values are sent between devices in bfloat16 or wider.
A program may use at most 1 GiB of HBM per device.

v0:
```python
import jax
import jax.numpy as jnp
from jax import lax
from jax.sharding import PartitionSpec as P


def solution(mesh):
    def local_transform(ao_rows, coeffs):
        local_rows = ao_rows.shape[0]
        n_basis = coeffs.shape[0]
        t_one = jnp.einsum('pqrs,rj->pqsj', ao_rows, coeffs, preferred_element_type=jnp.float32).astype(jnp.bfloat16)
        half_ints = jnp.einsum('pqsj,sb->pqjb', t_one, coeffs, preferred_element_type=jnp.float32).astype(jnp.bfloat16)
        h_flat = half_ints.reshape(local_rows, n_basis, n_basis * n_basis)
        full_pq = lax.all_to_all(h_flat, 'dev', split_axis=2, concat_axis=0, tiled=True)
        g_local = jnp.einsum('qa,pqk->apk', coeffs, full_pq, preferred_element_type=jnp.float32).astype(jnp.bfloat16)
        return jnp.einsum('pi,apk->iak', coeffs, g_local, preferred_element_type=jnp.float32)

    return jax.shard_map(local_transform, mesh=mesh, in_specs=(P(('frag', 'dev')), P('frag')), out_specs=P('frag', None, 'dev'), check_vma=False)
```

profile of v0, /device:TPU:1, one launch (start us, length us, event | category | flops | bytes accessed | tf_op | source)
XLA Modules:
  0.0 525.8 jit_solution(2528023140346736173)
XLA Ops:
  0.0 0.0 copy-start
  0.0 0.7 copy-done
  0.7 15.0 %fusion.6 = bf16[6,96,96,96]{3,2,1,0:T(8,128)(2,1)} fusion(bf16[6,96,96,96]{3,2,1,0:T(8,128)(2,1)} %param.2, bf16[96,96]{1,0:T(8,128)(2,1)S(1)} %copy-done), kind=kOutput, calls=%fused_computation.6 | convolution fusion | flops 2049048576 | bytes 21252096 | tf_op jit(solution)/shard_map/pqsj,sb->pqjb/dot_general | solution.py:12
  15.7 20.4 %copy.28 = bf16[6,96,96,96]{1,0,3,2:T(8,128)(2,1)} copy(bf16[6,96,96,96]{3,2,1,0:T(8,128)(2,1)} %fusion.6) | data formatting | bytes 21233664 | tf_op jit(solution)/shard_map/reshape | solution.py:13
  36.1 414.4 %all_to_all.18 = bf16[6,96,9216]{1,0,2:T(8,128)(2,1)} all-to-all(bf16[6,96,9216]{1,0,2:T(8,128)(2,1)} %bitcast.25), channel_id=1, replica_groups=mesh['frag'=2,'dev'=16] {'dev'}, dimensions={2} | all-to-all | bytes 21233664 | tf_op jit(solution)/shard_map/all_to_all | solution.py:14
  450.5 25.3 %copy.18 = bf16[16,6,96,576]{3,2,1,0:T(8,128)(2,1)} copy(bf16[16,6,96,576]{2,1,3,0:T(8,128)(2,1)} %bitcast.26) | data formatting | bytes 21233664 | tf_op jit(solution)/shard_map/all_to_all | solution.py:14
  475.8 11.9 %convert_bitcast_fusion = bf16[96,96,576]{2,0,1:T(8,128)(2,1)} fusion(bf16[96,96,576]{2,1,0:T(8,128)(2,1)} %bitcast.24, bf16[96,96]{1,0:T(8,128)(2,1)S(1)} %copy-done), kind=kOutput, calls=%fused_computation.4 | convolution fusion | flops 1024524288 | bytes 21252096 | tf_op jit(solution)/shard_map/qa,pqk->apk/dot_general | solution.py:15
  487.7 16.1 %fusion.9 = f32[96,96,576]{2,0,1:T(8,128)} fusion(bf16[96,96,576]{2,0,1:T(8,128)(2,1)} %convert_bitcast_fusion, bf16[96,96]{1,0:T(8,128)(2,1)S(1)} %copy-done), kind=kOutput, calls=%fused_computation.7 | convolution fusion | flops 1019215872 | bytes 31868928 | tf_op jit(solution)/shard_map/pi,apk->iak/dot_general | solution.py:16
  503.8 22.1 %copy.22 = f32[96,96,576]{2,1,0:T(8,128)} copy(f32[96,96,576]{2,0,1:T(8,128)} %fusion.9) | data formatting | bytes 42467328 | tf_op jit(solution)/shard_map/pi,apk->iak/dot_general | solution.py:16
Async XLA Ops:
  0.0 0.7 copy-start
where the time goes:
time: 528 us; the launch traced here: 526 us
  blocking collectives  414 us (78%)
  local copies, waits for them, and re-layouts  68.5 us (13%)
  matrix products  42.9 us (8%)
    all_to_all x1, blocking collectives, local_transform(): lax.all_to_all(h_flat, 'dev', split_axis=2, concat_axis=0, tiled=True)  414 us
    all_to_all x1, local copies, waits for them, and re-layouts, local_transform(): lax.all_to_all(h_flat, 'dev', split_axis=2, concat_axis=0, tiled=True)  25.3 us
    dot_general x1, local copies, waits for them, and re-layouts, local_transform(): jnp.einsum('pi,apk->iak', coeffs, g_local, preferred_element_type=jnp.flo...  22.1 us
    reshape x1, local copies, waits for them, and re-layouts, local_transform(): h_flat = half_ints.reshape(local_rows, n_basis, n_basis * n_basis)  20.4 us
    dot_general x1, matrix products, local_transform(): jnp.einsum('pi,apk->iak', coeffs, g_local, preferred_element_type=jnp.flo...  16.1 us
    dot_general x1, matrix products, local_transform(): jnp.einsum('pqsj,sb->pqjb', t_one, coeffs, preferred_element_type=jnp.flo...  15 us
    dot_general x1, matrix products, local_transform(): jnp.einsum('qa,pqk->apk', coeffs, full_pq, preferred_element_type=jnp.flo...  11.9 us

commit v1 on v0

v1 whole, which is shorter than its diff:
```python
import functools

import jax
import jax.numpy as jnp
from jax import lax
from jax.experimental import pallas as pl
from jax.experimental.pallas import tpu as pltpu
from jax.sharding import PartitionSpec as P

MESH = pl.DeviceIdType.MESH
N = 96
DEV = 16
PAIRS = 3
COLS = 6
QPAD = 104
QB = 8
TILES = 54


def iota(shape, dim):
    return lax.broadcasted_iota(jnp.int32, shape, dim)


def onehot(mask):
    return jnp.where(mask, 1.0, 0.0).astype(jnp.bfloat16)


def dot(x, y, dims=((1,), (0,))):
    return lax.dot_general(x, y, (dims, ((), ())), preferred_element_type=jnp.float32)


def exchange_kernel(a_hbm, c_ref, g_hbm, kc_ref, a_vm, h_scr, send, cc_ref, a_sem, send_sem, recv_sem, own_sem):
    frag = lax.axis_index('frag')
    me = lax.axis_index('dev')
    chip, core = me // 2, me % 2
    cz1, cz0, cy = chip // 4, (chip // 2) % 2, chip % 2

    def load(p, part):
        quarter = pl.ds(part * (N // 4), N // 4)
        return pltpu.make_async_copy(a_hbm.at[p, quarter], a_vm.at[p, quarter], a_sem.at[p, part])

    for p in range(2 * PAIRS):
        for part in range(4):
            load(p, part).start()

    barrier = pltpu.get_barrier_semaphore()

    @pl.loop(1, DEV)
    def _(k):
        pl.semaphore_signal(barrier, inc=1, device_id=(frag, (me + k) % DEV), device_id_type=MESH)

    c = c_ref[...]
    eye = onehot(iota((N, N), 0) == iota((N, N), 1))
    ct = dot(eye, c, ((1,), (1,))).astype(jnp.bfloat16)
    c_pad = dot(c, onehot(iota((N, 128), 0) == iota((N, 128), 1))).astype(jnp.bfloat16)
    row = iota((2 * N, N), 0)
    pick_a = onehot(iota((2 * N, N), 1) == 8 * (row // 16) + row % 8)
    c_rows = dot(pick_a, c, ((1,), (1,))).astype(jnp.bfloat16)
    wide = dot(c_rows, onehot(iota((N, 2 * N), 1) % N == iota((N, 2 * N), 0)))
    same_p = (iota((2 * N, 2 * N), 0) % 16) // 8 == iota((2 * N, 2 * N), 1) // N
    cc_ref[...] = jnp.where(same_p, wide, 0.0).astype(jnp.bfloat16)

    pl.semaphore_wait(barrier, DEV - 1)

    lane = iota((N, 128), 1)

    def copy_out(pp, dest):
        return pltpu.make_async_remote_copy(
            src_ref=send.at[pp, dest],
            dst_ref=g_hbm.at[me * PAIRS + pp],
            send_sem=send_sem.at[pp, dest],
            recv_sem=recv_sem.at[pp, me],
            device_id=(frag, dest),
            device_id_type=MESH,
        )

    def copy_own(pp):
        return pltpu.make_async_copy(send.at[pp, me], g_hbm.at[me * PAIRS + pp], own_sem.at[pp])

    def pack(pp, dest_chip):
        halves = []
        for p in range(2):
            tiles, last = [], []
            for cc in range(2):
                j0 = (dest_chip * 2 + cc) * COLS
                x = [h_scr[p, pl.ds(pl.multiple_of((j0 + l) * QPAD, 8), N), :] for l in range(COLS)]
                r1, r2, r3 = pltpu.roll(x[1], 96, 1), pltpu.roll(x[2], 64, 1), pltpu.roll(x[3], 32, 1)
                r5 = pltpu.roll(x[5], 96, 1)
                tiles += [jnp.where(lane < 96, x[0], r1), jnp.where(lane < 64, r1, r2),
                          jnp.where(lane < 32, r2, r3), jnp.where(lane < 96, x[4], r5)]
                last.append(r5 if cc == 0 else pltpu.roll(x[5], 32, 1))
            tiles.append(jnp.where(lane < 64, last[0], last[1]))
            halves.append(jnp.concatenate([t.astype(jnp.bfloat16) for t in tiles], axis=1))
        rhs = jnp.concatenate(halves, axis=0)
        out = dot(cc_ref[...], rhs)
        for cc in range(2):
            dest = dest_chip * 2 + cc
            for t in range(4):
                tile = out[:, (cc * 4 + t) * 128:(cc * 4 + t + 1) * 128].astype(jnp.bfloat16)
                for g in range(12):
                    send[pp, dest, g * 4 + t] = tile[g * 16:(g + 1) * 16]
        low = iota((16, 128), 1) < 64
        for u in range(6):
            upper = out[u * 32:u * 32 + 16, 1024:]
            lower = out[u * 32 + 16:u * 32 + 32, 1024:]
            send[pp, dest_chip * 2, 48 + u] = jnp.where(low, upper, pltpu.roll(lower, 64, 1)).astype(jnp.bfloat16)
            send[pp, dest_chip * 2 + 1, 48 + u] = jnp.where(low, pltpu.roll(upper, 64, 1), lower).astype(jnp.bfloat16)

    @pl.loop(0, PAIRS)
    def _(pp):
        for p2 in range(2):
            p = pp * 2 + p2
            for part in range(4):
                load(p, part).wait()

                @pl.loop(0, N // 4 // QB)
                def _(qb):
                    q0 = part * (N // 4) + qb * QB
                    t_rows = [dot(ct, a_vm[p, q0 + i]).astype(jnp.bfloat16) for i in range(QB)]
                    half = dot(jnp.concatenate(t_rows, axis=0), c_pad)
                    for i in range(QB):
                        h_scr[p2, pl.ds(q0 + i, N, stride=QPAD), :] = half[i * N:(i + 1) * N]

        @pl.loop(0, 7)
        def _(t):
            m = 7 - t
            dest_chip = 4 * ((cz1 + m // 4) % 2) + 2 * ((cz0 + (m // 2) % 2) % 2) + (cy + m % 2) % 2
            pack(pp, dest_chip)
            copy_out(pp, dest_chip * 2).start()
            copy_out(pp, dest_chip * 2 + 1).start()

        pack(pp, chip)
        copy_out(pp, chip * 2 + 1 - core).start()
        copy_own(pp).start()

    m8 = 8 * N
    spread = dot(onehot(iota((m8, N), 0) // 8 == iota((m8, N), 1)), c, ((1,), (1,))).astype(jnp.bfloat16)
    full = dot(spread, onehot(iota((N, m8), 1) // 8 == iota((N, m8), 0)))
    same = iota((m8, m8), 0) % 8 == iota((m8, m8), 1) % 8
    kc_ref[...] = jnp.where(same, full, 0.0).astype(jnp.bfloat16)

    @pl.loop(0, PAIRS)
    def _(pp):
        copy_own(pp).wait()

        @pl.loop(1, DEV)
        def _(k):
            copy_out(pp, (me + k) % DEV).wait_send()

        @pl.loop(1, DEV)
        def _(k):
            src = (me + k) % DEV
            pltpu.make_async_remote_copy(
                src_ref=send.at[pp, src], dst_ref=g_hbm.at[src * PAIRS + pp],
                send_sem=send_sem.at[pp, src], recv_sem=recv_sem.at[pp, src],
                device_id=(frag, src), device_id_type=MESH,
            ).wait_recv()


def last_kernel(main_ref, half_ref, kc_ref, v_ref):
    kc = kc_ref[...]
    k = 8 * N
    for gg in range(2):
        for n in range(2):
            rhs = jnp.concatenate([main_ref[:, gg * 4 + 2 * n + t].reshape(k, 128) for t in range(2)], axis=1)
            out = dot(kc, rhs)
            v_ref[:, gg * 8:(gg + 1) * 8, n * 256:(n + 1) * 256] = out.reshape(N, 8, 256)
    out = dot(kc, half_ref[:, 0].reshape(k, 128))
    v_ref[:, 0:8, 512:576] = out.reshape(N, 8, 128)[:, :, :64]
    v_ref[:, 8:16, 512:576] = pltpu.roll(out, 64, 1).reshape(N, 8, 128)[:, :, :64]


def solution(mesh):
    def local_transform(ao_rows, coeffs):
        blocks = DEV * PAIRS
        g_all, kc = pl.pallas_call(
            exchange_kernel,
            out_shape=(jax.ShapeDtypeStruct((blocks, TILES, 16, 128), jnp.bfloat16),
                       jax.ShapeDtypeStruct((8 * N, 8 * N), jnp.bfloat16)),
            in_specs=[pl.BlockSpec(memory_space=pltpu.HBM), pl.BlockSpec(memory_space=pltpu.VMEM)],
            out_specs=(pl.BlockSpec(memory_space=pltpu.HBM), pl.BlockSpec(memory_space=pltpu.VMEM)),
            scratch_shapes=[
                pltpu.VMEM((2 * PAIRS, N, N, N), jnp.bfloat16),
                pltpu.VMEM((2, N * QPAD, 128), jnp.float32),
                pltpu.VMEM((PAIRS, DEV, TILES, 16, 128), jnp.bfloat16),
                pltpu.VMEM((2 * N, 2 * N), jnp.bfloat16),
                pltpu.SemaphoreType.DMA((2 * PAIRS, 4)),
                pltpu.SemaphoreType.DMA((PAIRS, DEV)),
                pltpu.SemaphoreType.DMA((PAIRS, DEV)),
                pltpu.SemaphoreType.DMA((PAIRS,)),
            ],
            compiler_params=pltpu.CompilerParams(collective_id=0, has_side_effects=True, vmem_limit_bytes=60 * 2**20),
            cost_estimate=pl.CostEstimate(flops=6 * 10**9, bytes_accessed=40 * 10**6, transcendentals=0),
            name='exchange',
        )(ao_rows, coeffs)
        return pl.pallas_call(
            last_kernel,
            grid=(6,),
            out_shape=jax.ShapeDtypeStruct((N, N, COLS * N), jnp.float32),
            in_specs=[
                pl.BlockSpec((blocks, 8, 16, 128), lambda u: (0, u, 0, 0)),
                pl.BlockSpec((blocks, 1, 16, 128), lambda u: (0, 48 + u, 0, 0)),
                pl.BlockSpec((8 * N, 8 * N), lambda u: (0, 0)),
            ],
            out_specs=pl.BlockSpec((N, 16, COLS * N), lambda u: (0, u, 0)),
            compiler_params=pltpu.CompilerParams(vmem_limit_bytes=48 * 2**20),
            cost_estimate=pl.CostEstimate(flops=8 * 10**9, bytes_accessed=35 * 10**6, transcendentals=0),
            name='last_product',
        )(g_all, g_all, kc)

    return jax.shard_map(local_transform, mesh=mesh, in_specs=(P(('frag', 'dev')), P('frag')), out_specs=P('frag', None, 'dev'), check_vma=False)
```

time: 528 us -> 278 us (0.53)
  blocking collectives: 414 us -> 0 us
  Pallas kernels: 0 us -> 277 us
  local copies, waits for them, and re-layouts: 68.5 us -> 1.26 us
  matrix products: 42.9 us -> 0 us
    all_to_all x1 -> x0, blocking collectives: 414 us -> none  [local_transform(): lax.all_to_all(h_flat, 'dev', split_axis=2, concat_axis=0, tiled=True)]
    pallas_call x0 -> x2, Pallas kernels: none -> 277 us  [the longest x1 260 us: local_transform(): pl.pallas_call(exchange_kernel, out_shape=(jax.ShapeDtypeStruct((blocks,...]
    dot_general x3 -> x0, matrix products: 42.9 us -> none  [the longest x1 16.1 us: local_transform(): jnp.einsum('pi,apk->iak', coeffs, g_local, preferred_element_type=jnp.flo...]
    all_to_all x1 -> x0, local copies, waits for them, and re-layouts: 25.3 us -> none  [local_transform(): lax.all_to_all(h_flat, 'dev', split_axis=2, concat_axis=0, tiled=True)]
    dot_general x1 -> x0, local copies, waits for them, and re-layouts: 22.1 us -> none  [local_transform(): jnp.einsum('pi,apk->iak', coeffs, g_local, preferred_element_type=jnp.flo...]
    reshape x1 -> x0, local copies, waits for them, and re-layouts: 20.4 us -> none  [local_transform(): h_flat = half_ints.reshape(local_rows, n_basis, n_basis * n_basis)]
where the time goes in v1:
time: 278 us
  Pallas kernels  277 us (100%)
    pallas_call x1, Pallas kernels, local_transform(): pl.pallas_call(exchange_kernel, out_shape=(jax.ShapeDtypeStruct((blocks,...  260 us
    pallas_call x1, Pallas kernels, local_transform(): pl.pallas_call(last_kernel, grid=(6,), out_shape=jax.ShapeDtypeStruct((N,...  16.4 us

profile of v1, /device:TPU:1, one launch (start us, length us, event | category | flops | bytes accessed | tf_op | source)
XLA Modules:
  0.0 277.9 jit_solution(2368313816263879966)
XLA Ops:
  0.0 260.3 %exchange.1 = (bf16[48,54,16,128]{3,2,1,0:T(8,128)(2,1)}, bf16[768,768]{1,0:T(8,128)(2,1)}) custom-call(bf16[6,96,96,96]{3,2,1,0:T(8,128)(2,1)} %a_hbm.1, bf16[96,96]{1,0:T(8,128)(2,1)} %c_ref.1), custom_call_target="tpu_custom_call" | custom-call | flops 6000000000 | bytes 40000000 | tf_op jit(solution)/shard_map/exchange/pallas_call | solution.py:176
  260.3 0.0 copy-start
  260.3 1.3 copy-done
  261.6 16.4 %last_product.1 = f32[96,96,576]{2,1,0:T(8,128)} custom-call(bf16[48,54,16,128]{3,2,1,0:T(8,128)(2,1)} %get-tuple-element.7.main_ref.half_ref, bf16[48,54,16,128]{3,2,1,0:T(8,128)(2,1)} %get-tuple-element.7.main_ref.half_ref, bf16[768,768]{1,0:T(8,128)(2,1)S(1)} %copy-done), custom_call_target="tpu_custom_call" | custom-call | flops 8000000000 | bytes 35000000 | tf_op jit(solution)/shard_map/last_product/pallas_call | solution.py:196
Async XLA Ops:
  260.3 1.3 copy-start

commit v2 on v1

--- a/solution.py
+++ b/solution.py
@@ -29,16 +29,19 @@
     return lax.dot_general(x, y, (dims, ((), ())), preferred_element_type=jnp.float32)
 
 
-def exchange_kernel(a_hbm, c_ref, g_hbm, kc_ref, a_vm, h_scr, send, cc_ref, a_sem, send_sem, recv_sem, own_sem):
+def exchange_kernel(a_hbm, c_hbm, g_hbm, kc_ref, a_vm, c_vm, h_scr, send, cc_ref, a_sem, c_sem, send_sem, recv_sem, own_sem):
     frag = lax.axis_index('frag')
     me = lax.axis_index('dev')
     chip, core = me // 2, me % 2
     cz1, cz0, cy = chip // 4, (chip // 2) % 2, chip % 2
+    edge = 1 - (cz1 + cz0) % 2
 
     def load(p, part):
         quarter = pl.ds(part * (N // 4), N // 4)
         return pltpu.make_async_copy(a_hbm.at[p, quarter], a_vm.at[p, quarter], a_sem.at[p, part])
 
+    load_c = pltpu.make_async_copy(c_hbm, c_vm, c_sem)
+    load_c.start()
     for p in range(2 * PAIRS):
         for part in range(4):
             load(p, part).start()
@@ -49,10 +52,15 @@
     def _(k):
         pl.semaphore_signal(barrier, inc=1, device_id=(frag, (me + k) % DEV), device_id_type=MESH)
 
-    c = c_ref[...]
+    load_c.wait()
+    c = c_vm[...]
     eye = onehot(iota((N, N), 0) == iota((N, N), 1))
     ct = dot(eye, c, ((1,), (1,))).astype(jnp.bfloat16)
-    c_pad = dot(c, onehot(iota((N, 128), 0) == iota((N, 128), 1))).astype(jnp.bfloat16)
+    r2, c2 = iota((256, N), 0), iota((N, 256), 1)
+    stacked = dot(onehot(r2 % 128 == iota((256, N), 1)), c).astype(jnp.bfloat16)
+    both = dot(stacked, onehot(c2 % 128 == iota((N, 256), 0)))
+    c_two = jnp.where(iota((256, 256), 0) // 128 == iota((256, 256), 1) // 128, both, 0.0).astype(jnp.bfloat16)
+    gap = jnp.zeros((N, 32), jnp.bfloat16)
     row = iota((2 * N, N), 0)
     pick_a = onehot(iota((2 * N, N), 1) == 8 * (row // 16) + row % 8)
     c_rows = dot(pick_a, c, ((1,), (1,))).astype(jnp.bfloat16)
@@ -116,22 +124,30 @@
                 @pl.loop(0, N // 4 // QB)
                 def _(qb):
                     q0 = part * (N // 4) + qb * QB
-                    t_rows = [dot(ct, a_vm[p, q0 + i]).astype(jnp.bfloat16) for i in range(QB)]
-                    half = dot(jnp.concatenate(t_rows, axis=0), c_pad)
+                    t_rows = []
+                    for i in range(0, QB, 2):
+                        two = jnp.concatenate([a_vm[p, q0 + i], gap, a_vm[p, q0 + i + 1], gap], axis=1)
+                        t_rows.append(dot(ct, two).astype(jnp.bfloat16))
+                    half = dot(jnp.concatenate(t_rows, axis=0), c_two)
                     for i in range(QB):
-                        h_scr[p2, pl.ds(q0 + i, N, stride=QPAD), :] = half[i * N:(i + 1) * N]
-
-        @pl.loop(0, 7)
+                        rows = half[(i // 2) * N:(i // 2 + 1) * N, (i % 2) * 128:(i % 2 + 1) * 128]
+                        h_scr[p2, pl.ds(q0 + i, N, stride=QPAD), :] = rows
+
+        @pl.loop(0, 8)
         def _(t):
-            m = 7 - t
+            m = (7 - t + 4 * edge) % 8
             dest_chip = 4 * ((cz1 + m // 4) % 2) + 2 * ((cz0 + (m // 2) % 2) % 2) + (cy + m % 2) % 2
             pack(pp, dest_chip)
-            copy_out(pp, dest_chip * 2).start()
-            copy_out(pp, dest_chip * 2 + 1).start()
-
-        pack(pp, chip)
-        copy_out(pp, chip * 2 + 1 - core).start()
-        copy_own(pp).start()
+            for cc in range(2):
+                dest = dest_chip * 2 + cc
+
+                @pl.when(dest != me)
+                def _():
+                    copy_out(pp, dest).start()
+
+                @pl.when(dest == me)
+                def _():
+                    copy_own(pp).start()
 
     m8 = 8 * N
     spread = dot(onehot(iota((m8, N), 0) // 8 == iota((m8, N), 1)), c, ((1,), (1,))).astype(jnp.bfloat16)
@@ -177,19 +193,21 @@
             exchange_kernel,
             out_shape=(jax.ShapeDtypeStruct((blocks, TILES, 16, 128), jnp.bfloat16),
                        jax.ShapeDtypeStruct((8 * N, 8 * N), jnp.bfloat16)),
-            in_specs=[pl.BlockSpec(memory_space=pltpu.HBM), pl.BlockSpec(memory_space=pltpu.VMEM)],
-            out_specs=(pl.BlockSpec(memory_space=pltpu.HBM), pl.BlockSpec(memory_space=pltpu.VMEM)),
+            in_specs=[pl.BlockSpec(memory_space=pltpu.HBM), pl.BlockSpec(memory_space=pltpu.HBM)],
+            out_specs=(pl.BlockSpec(memory_space=pl.ANY), pl.BlockSpec(memory_space=pltpu.VMEM)),
             scratch_shapes=[
                 pltpu.VMEM((2 * PAIRS, N, N, N), jnp.bfloat16),
+                pltpu.VMEM((N, N), jnp.bfloat16),
                 pltpu.VMEM((2, N * QPAD, 128), jnp.float32),
                 pltpu.VMEM((PAIRS, DEV, TILES, 16, 128), jnp.bfloat16),
                 pltpu.VMEM((2 * N, 2 * N), jnp.bfloat16),
                 pltpu.SemaphoreType.DMA((2 * PAIRS, 4)),
+                pltpu.SemaphoreType.DMA,
                 pltpu.SemaphoreType.DMA((PAIRS, DEV)),
                 pltpu.SemaphoreType.DMA((PAIRS, DEV)),
                 pltpu.SemaphoreType.DMA((PAIRS,)),
             ],
-            compiler_params=pltpu.CompilerParams(collective_id=0, has_side_effects=True, vmem_limit_bytes=60 * 2**20),
+            compiler_params=pltpu.CompilerParams(collective_id=0, has_side_effects=True, vmem_limit_bytes=41 * 2**20),
             cost_estimate=pl.CostEstimate(flops=6 * 10**9, bytes_accessed=40 * 10**6, transcendentals=0),
             name='exchange',
         )(ao_rows, coeffs)
@@ -203,7 +221,7 @@
                 pl.BlockSpec((8 * N, 8 * N), lambda u: (0, 0)),
             ],
             out_specs=pl.BlockSpec((N, 16, COLS * N), lambda u: (0, u, 0)),
-            compiler_params=pltpu.CompilerParams(vmem_limit_bytes=48 * 2**20),
+            compiler_params=pltpu.CompilerParams(vmem_limit_bytes=20 * 2**20),
             cost_estimate=pl.CostEstimate(flops=8 * 10**9, bytes_accessed=35 * 10**6, transcendentals=0),
             name='last_product',
         )(g_all, g_all, kc)

time: 278 us -> 274 us (0.986)
  Pallas kernels: 277 us -> 273 us
where the time goes in v2:
time: 274 us
  Pallas kernels  273 us (100%)
    pallas_call x1, Pallas kernels, local_transform(): pl.pallas_call(exchange_kernel, out_shape=(jax.ShapeDtypeStruct((blocks,...  259 us
    pallas_call x1, Pallas kernels, local_transform(): pl.pallas_call(last_kernel, grid=(6,), out_shape=jax.ShapeDtypeStruct((N,...  14.8 us

profile of v2, /device:TPU:1, one launch (start us, length us, event | category | flops | bytes accessed | tf_op | source)
XLA Modules:
  0.0 274.0 jit_solution(9256341164175774395)
XLA Ops:
  0.0 0.0 copy-start
  0.0 0.7 copy-done
  0.7 258.5 %exchange.1 = (bf16[48,54,16,128]{3,2,1,0:T(8,128)(2,1)S(1)}, bf16[768,768]{1,0:T(8,128)(2,1)S(1)}) custom-call(bf16[6,96,96,96]{3,2,1,0:T(8,128)(2,1)} %a_hbm.1, bf16[96,96]{1,0:T(8,128)(2,1)S(1)} %copy-done), custom_call_target="tpu_custom_call" | custom-call | flops 6000000000 | bytes 40000000 | tf_op jit(solution)/shard_map/exchange/pallas_call | solution.py:192
  259.2 14.8 %last_product.1 = f32[96,96,576]{2,1,0:T(8,128)} custom-call(bf16[48,54,16,128]{3,2,1,0:T(8,128)(2,1)S(1)} %get-tuple-element.7.main_ref.half_ref, bf16[48,54,16,128]{3,2,1,0:T(8,128)(2,1)S(1)} %get-tuple-element.7.main_ref.half_ref, bf16[768,768]{1,0:T(8,128)(2,1)S(1)} %get-tuple-element.8.kc_ref), custom_call_target="tpu_custom_call" | custom-call | flops 8000000000 | bytes 35000000 | tf_op jit(solution)/shard_map/last_product/pallas_call | solution.py:214
Async XLA Ops:
  0.0 0.7 copy-start

commit v3 on v2

--- a/solution.py
+++ b/solution.py
@@ -81,6 +81,15 @@
             device_id=(frag, dest),
             device_id_type=MESH,
         )
+
+    def chip_at(m):
+        return 4 * ((cz1 + m // 4) % 2) + 2 * ((cz0 + (m // 2) % 2) % 2) + (cy + m % 2) % 2
+
+    def far(n):
+        return copy_out(n // 8, chip_at(7 - (n // 2) % 4) * 2 + n % 2)
+
+    def near(n):
+        return copy_out(n // 4, chip_at(3 - (n // 2) % 2) * 2 + n % 2)
 
     def copy_own(pp):
         return pltpu.make_async_copy(send.at[pp, me], g_hbm.at[me * PAIRS + pp], own_sem.at[pp])
@@ -136,12 +145,13 @@
         @pl.loop(0, 8)
         def _(t):
             m = (7 - t + 4 * edge) % 8
-            dest_chip = 4 * ((cz1 + m // 4) % 2) + 2 * ((cz0 + (m // 2) % 2) % 2) + (cy + m % 2) % 2
+            dest_chip = chip_at(m)
             pack(pp, dest_chip)
+            later = (1 - edge) * (m // 2) == 1
             for cc in range(2):
                 dest = dest_chip * 2 + cc
 
-                @pl.when(dest != me)
+                @pl.when(jnp.logical_and(dest != me, jnp.logical_not(later)))
                 def _():
                     copy_out(pp, dest).start()
 
@@ -155,13 +165,30 @@
     same = iota((m8, m8), 0) % 8 == iota((m8, m8), 1) % 8
     kc_ref[...] = jnp.where(same, full, 0.0).astype(jnp.bfloat16)
 
+    @pl.loop(0, 4 * PAIRS)
+    def _(n):
+        @pl.when(jnp.logical_and(edge == 0, core == 0))
+        def _():
+            near(n).start()
+
+        far(2 * n).wait_send()
+
+        @pl.when(jnp.logical_and(edge == 0, core == 1))
+        def _():
+            near(n).start()
+
+        far(2 * n + 1).wait_send()
+
     @pl.loop(0, PAIRS)
     def _(pp):
         copy_own(pp).wait()
-
-        @pl.loop(1, DEV)
-        def _(k):
-            copy_out(pp, (me + k) % DEV).wait_send()
+        copy_out(pp, chip * 2 + 1 - core).wait_send()
+        copy_out(pp, chip_at(1) * 2).wait_send()
+        copy_out(pp, chip_at(1) * 2 + 1).wait_send()
+
+        @pl.loop(0, 4)
+        def _(n):
+            near(4 * pp + n).wait_send()
 
         @pl.loop(1, DEV)
         def _(k):

time: 274 us -> 284 us (1.036)
  Pallas kernels: 273 us -> 283 us
    pallas_call x1, Pallas kernels: 259 us -> 268 us  [local_transform(): pl.pallas_call(exchange_kernel, out_shape=(jax.ShapeDtypeStruct((blocks,...]
where the time goes in v3:
time: 284 us; the launch traced here: 283 us
  Pallas kernels  283 us (100%)
    pallas_call x1, Pallas kernels, local_transform(): pl.pallas_call(exchange_kernel, out_shape=(jax.ShapeDtypeStruct((blocks,...  268 us
    pallas_call x1, Pallas kernels, local_transform(): pl.pallas_call(last_kernel, grid=(6,), out_shape=jax.ShapeDtypeStruct((N,...  14.8 us

profile of v3, /device:TPU:1, one launch (start us, length us, event | category | flops | bytes accessed | tf_op | source)
XLA Modules:
  0.0 283.4 jit_solution(7689578367428305733)
XLA Ops:
  0.0 0.0 copy-start
  0.0 0.7 copy-done
  0.7 267.9 %exchange.1 = (bf16[48,54,16,128]{3,2,1,0:T(8,128)(2,1)S(1)}, bf16[768,768]{1,0:T(8,128)(2,1)S(1)}) custom-call(bf16[6,96,96,96]{3,2,1,0:T(8,128)(2,1)} %a_hbm.1, bf16[96,96]{1,0:T(8,128)(2,1)S(1)} %copy-done), custom_call_target="tpu_custom_call" | custom-call | flops 6000000000 | bytes 40000000 | tf_op jit(solution)/shard_map/exchange/pallas_call | solution.py:219
  268.7 14.8 %last_product.1 = f32[96,96,576]{2,1,0:T(8,128)} custom-call(bf16[48,54,16,128]{3,2,1,0:T(8,128)(2,1)S(1)} %get-tuple-element.7.main_ref.half_ref, bf16[48,54,16,128]{3,2,1,0:T(8,128)(2,1)S(1)} %get-tuple-element.7.main_ref.half_ref, bf16[768,768]{1,0:T(8,128)(2,1)S(1)} %get-tuple-element.8.kc_ref), custom_call_target="tpu_custom_call" | custom-call | flops 8000000000 | bytes 35000000 | tf_op jit(solution)/shard_map/last_product/pallas_call | solution.py:241
Async XLA Ops:
  0.0 0.7 copy-start

commit v4 on v2

--- a/solution.py
+++ b/solution.py
@@ -15,6 +15,8 @@
 QPAD = 104
 QB = 8
 TILES = 54
+PART = 9
+GROUPS = ((7, 4, 3, 1), (6, 5, 2, 0))
 
 
 def iota(shape, dim):
@@ -34,7 +36,6 @@
     me = lax.axis_index('dev')
     chip, core = me // 2, me % 2
     cz1, cz0, cy = chip // 4, (chip // 2) % 2, chip % 2
-    edge = 1 - (cz1 + cz0) % 2
 
     def load(p, part):
         quarter = pl.ds(part * (N // 4), N // 4)
@@ -72,10 +73,14 @@
 
     lane = iota((N, 128), 1)
 
-    def copy_out(pp, dest):
+    def chip_at(m):
+        return 4 * ((cz1 + m // 4) % 2) + 2 * ((cz0 + (m // 2) % 2) % 2) + (cy + m % 2) % 2
+
+    def copy_out(pp, dest, part=None):
+        tiles = pl.ds(0, TILES) if part is None else pl.ds(part * PART, PART)
         return pltpu.make_async_remote_copy(
-            src_ref=send.at[pp, dest],
-            dst_ref=g_hbm.at[me * PAIRS + pp],
+            src_ref=send.at[pp, dest, tiles],
+            dst_ref=g_hbm.at[me * PAIRS + pp, tiles],
             send_sem=send_sem.at[pp, dest],
             recv_sem=recv_sem.at[pp, me],
             device_id=(frag, dest),
@@ -133,21 +138,20 @@
                         rows = half[(i // 2) * N:(i // 2 + 1) * N, (i % 2) * 128:(i % 2 + 1) * 128]
                         h_scr[p2, pl.ds(q0 + i, N, stride=QPAD), :] = rows
 
-        @pl.loop(0, 8)
-        def _(t):
-            m = (7 - t + 4 * edge) % 8
-            dest_chip = 4 * ((cz1 + m // 4) % 2) + 2 * ((cz0 + (m // 2) % 2) % 2) + (cy + m % 2) % 2
-            pack(pp, dest_chip)
-            for cc in range(2):
-                dest = dest_chip * 2 + cc
-
-                @pl.when(dest != me)
-                def _():
-                    copy_out(pp, dest).start()
-
-                @pl.when(dest == me)
-                def _():
-                    copy_own(pp).start()
+        for group in GROUPS:
+            for m in group:
+                pack(pp, chip_at(m))
+
+            @pl.loop(0, TILES // PART)
+            def _(part):
+                for cc in range(2):
+                    for m in group:
+                        if m > 0:
+                            copy_out(pp, chip_at(m) * 2 + cc, part).start()
+                        elif cc == 1:
+                            copy_out(pp, chip * 2 + 1 - core, part).start()
+
+        copy_own(pp).start()
 
     m8 = 8 * N
     spread = dot(onehot(iota((m8, N), 0) // 8 == iota((m8, N), 1)), c, ((1,), (1,))).astype(jnp.bfloat16)

time: 274 us -> 262 us (0.956)
  Pallas kernels: 273 us -> 261 us
    pallas_call x1, Pallas kernels: 259 us -> 246 us  [local_transform(): pl.pallas_call(exchange_kernel, out_shape=(jax.ShapeDtypeStruct((blocks,...]
where the time goes in v4:
time: 262 us
  Pallas kernels  261 us (100%)
    pallas_call x1, Pallas kernels, local_transform(): pl.pallas_call(exchange_kernel, out_shape=(jax.ShapeDtypeStruct((blocks,...  246 us
    pallas_call x1, Pallas kernels, local_transform(): pl.pallas_call(last_kernel, grid=(6,), out_shape=jax.ShapeDtypeStruct((N,...  14.8 us

profile of v4, /device:TPU:1, one launch (start us, length us, event | category | flops | bytes accessed | tf_op | source)
XLA Modules:
  0.0 261.9 jit_solution(8576630122330361715)
XLA Ops:
  0.0 0.0 copy-start
  0.0 0.7 copy-done
  0.7 246.4 %exchange.1 = (bf16[48,54,16,128]{3,2,1,0:T(8,128)(2,1)S(1)}, bf16[768,768]{1,0:T(8,128)(2,1)S(1)}) custom-call(bf16[6,96,96,96]{3,2,1,0:T(8,128)(2,1)} %a_hbm.1, bf16[96,96]{1,0:T(8,128)(2,1)S(1)} %copy-done), custom_call_target="tpu_custom_call" | custom-call | flops 6000000000 | bytes 40000000 | tf_op jit(solution)/shard_map/exchange/pallas_call | solution.py:196
  247.1 14.8 %last_product.1 = f32[96,96,576]{2,1,0:T(8,128)} custom-call(bf16[48,54,16,128]{3,2,1,0:T(8,128)(2,1)S(1)} %get-tuple-element.7.main_ref.half_ref, bf16[48,54,16,128]{3,2,1,0:T(8,128)(2,1)S(1)} %get-tuple-element.7.main_ref.half_ref, bf16[768,768]{1,0:T(8,128)(2,1)S(1)} %get-tuple-element.8.kc_ref), custom_call_target="tpu_custom_call" | custom-call | flops 8000000000 | bytes 35000000 | tf_op jit(solution)/shard_map/last_product/pallas_call | solution.py:218
Async XLA Ops:
  0.0 0.7 copy-start

commit v5 on v4

v5 whole, which is shorter than its diff:
```python
import jax
import jax.numpy as jnp
from jax import lax
from jax.experimental import pallas as pl
from jax.experimental.pallas import tpu as pltpu
from jax.sharding import PartitionSpec as P

MESH = pl.DeviceIdType.MESH
N = 96
DEV = 16
PAIRS = 3
COLS = 6
QPAD = 104
QB = 24
TILES = 54
PART = 9
K8 = 8 * N
KP = 16 * DEV
FIRST_GROUPS = ((7, 4), (6, 5), (3, 1), (2, 0))
LATER_GROUPS = ((7, 4, 3, 1, 6, 5, 2, 0),)


def iota(shape, dim):
    return lax.broadcasted_iota(jnp.int32, shape, dim)


def onehot(mask):
    return jnp.where(mask, 1.0, 0.0).astype(jnp.bfloat16)


def dot(x, y, dims=((1,), (0,))):
    return lax.dot_general(x, y, (dims, ((), ())), preferred_element_type=jnp.float32)


def exchange_kernel(a_hbm, c_hbm, g_last, vm0_ref, vm1_ref, vm2_ref, vh_ref, kc_ref,
                    a_vm, c_vm, h_scr, send, g_first, cc_ref, kc_first, a_sem, c_sem, send_sem, recv_sem, own_sem):
    frag = lax.axis_index('frag')
    me = lax.axis_index('dev')
    chip, core = me // 2, me % 2
    cz1, cz0, cy = chip // 4, (chip // 2) % 2, chip % 2

    def load(pp, idx):
        p2, quarter = idx // 4, pl.ds((idx % 4) * QB, QB)
        return pltpu.make_async_copy(a_hbm.at[2 * pp + p2, quarter], a_vm.at[p2, quarter], a_sem.at[idx])

    load_c = pltpu.make_async_copy(c_hbm, c_vm, c_sem)
    load_c.start()
    for idx in range(8):
        load(0, idx).start()

    barrier = pltpu.get_barrier_semaphore()

    @pl.loop(1, DEV)
    def _(k):
        pl.semaphore_signal(barrier, inc=1, device_id=(frag, (me + k) % DEV), device_id_type=MESH)

    load_c.wait()
    c = c_vm[...]
    eye = onehot(iota((N, N), 0) == iota((N, N), 1))
    ct = dot(eye, c, ((1,), (1,))).astype(jnp.bfloat16)
    stacked = dot(onehot(iota((256, N), 0) % 128 == iota((256, N), 1)), c).astype(jnp.bfloat16)
    both = dot(stacked, onehot(iota((N, 256), 1) % 128 == iota((N, 256), 0)))
    c_two = jnp.where(iota((256, 256), 0) // 128 == iota((256, 256), 1) // 128, both, 0.0).astype(jnp.bfloat16)
    gap = jnp.zeros((N, 32), jnp.bfloat16)
    row = iota((2 * N, N), 0)
    pick_a = onehot(iota((2 * N, N), 1) == 8 * (row // 16) + row % 8)
    c_rows = dot(pick_a, c, ((1,), (1,))).astype(jnp.bfloat16)
    wide = dot(c_rows, onehot(iota((N, 2 * N), 1) % N == iota((N, 2 * N), 0)))
    same_p = (iota((2 * N, 2 * N), 0) % 16) // 8 == iota((2 * N, 2 * N), 1) // N
    cc_ref[...] = jnp.where(same_p, wide, 0.0).astype(jnp.bfloat16)

    lane = iota((N, 128), 1)

    def chip_at(m):
        return 4 * ((cz1 + m // 4) % 2) + 2 * ((cz0 + (m // 2) % 2) % 2) + (cy + m % 2) % 2

    def block(pp, src, tiles):
        if isinstance(pp, int) and pp == PAIRS - 1:
            return g_last.at[src, tiles]
        return g_first.at[pp, src, tiles]

    def copy_out(pp, dest, part=None):
        tiles = pl.ds(0, TILES) if part is None else pl.ds(part * PART, PART)
        return pltpu.make_async_remote_copy(
            src_ref=send.at[pp, dest, tiles],
            dst_ref=block(pp, me, tiles),
            send_sem=send_sem.at[pp, dest],
            recv_sem=recv_sem.at[pp, me],
            device_id=(frag, dest),
            device_id_type=MESH,
        )

    def wait_recv(pp, src):
        tiles = pl.ds(0, TILES)
        pltpu.make_async_remote_copy(
            src_ref=send.at[pp, src, tiles], dst_ref=block(pp, src, tiles),
            send_sem=send_sem.at[pp, src], recv_sem=recv_sem.at[pp, src],
            device_id=(frag, src), device_id_type=MESH,
        ).wait_recv()

    def half_transform(pp):
        @pl.loop(0, 8)
        def _(idx):
            load(pp, idx).wait()
            p2, q0 = idx // 4, (idx % 4) * QB
            t_rows = []
            for i in range(0, QB, 2):
                two = jnp.concatenate([a_vm[p2, q0 + i], gap, a_vm[p2, q0 + i + 1], gap], axis=1)
                t_rows.append(dot(ct, two).astype(jnp.bfloat16))
            half = dot(jnp.concatenate(t_rows, axis=0), c_two)
            for i in range(QB):
                rows = half[(i // 2) * N:(i // 2 + 1) * N, (i % 2) * 128:(i % 2 + 1) * 128]
                h_scr[p2, pl.ds(q0 + i, N, stride=QPAD), :] = rows

    def pack(pp, dest_chip):
        halves = []
        for p in range(2):
            tiles, last = [], []
            for cc in range(2):
                j0 = (dest_chip * 2 + cc) * COLS
                x = [h_scr[p, pl.ds(pl.multiple_of((j0 + l) * QPAD, 8), N), :] for l in range(COLS)]
                r1, r2, r3 = pltpu.roll(x[1], 96, 1), pltpu.roll(x[2], 64, 1), pltpu.roll(x[3], 32, 1)
                r5 = pltpu.roll(x[5], 96, 1)
                tiles += [jnp.where(lane < 96, x[0], r1), jnp.where(lane < 64, r1, r2),
                          jnp.where(lane < 32, r2, r3), jnp.where(lane < 96, x[4], r5)]
                last.append(r5 if cc == 0 else pltpu.roll(x[5], 32, 1))
            tiles.append(jnp.where(lane < 64, last[0], last[1]))
            halves.append(jnp.concatenate([t.astype(jnp.bfloat16) for t in tiles], axis=1))
        out = dot(cc_ref[...], jnp.concatenate(halves, axis=0))
        for cc in range(2):
            dest = dest_chip * 2 + cc
            for t in range(4):
                tile = out[:, (cc * 4 + t) * 128:(cc * 4 + t + 1) * 128].astype(jnp.bfloat16)
                for g in range(12):
                    send[pp, dest, g * 4 + t] = tile[g * 16:(g + 1) * 16]
        low = iota((16, 128), 1) < 64
        for u in range(6):
            upper = out[u * 32:u * 32 + 16, 1024:]
            lower = out[u * 32 + 16:u * 32 + 32, 1024:]
            send[pp, dest_chip * 2, 48 + u] = jnp.where(low, upper, pltpu.roll(lower, 64, 1)).astype(jnp.bfloat16)
            send[pp, dest_chip * 2 + 1, 48 + u] = jnp.where(low, pltpu.roll(upper, 64, 1), lower).astype(jnp.bfloat16)

    def send_groups(pp, groups):
        for group in groups:
            for m in group:
                pack(pp, chip_at(m))

            @pl.loop(0, TILES // PART)
            def _(part):
                for cc in range(2):
                    for m in group:
                        if m > 0:
                            copy_out(pp, chip_at(m) * 2 + cc, part).start()
                        elif cc == 1:
                            copy_out(pp, chip * 2 + 1 - core, part).start()

    def copy_own(pp):
        return pltpu.make_async_copy(send.at[pp, me], block(pp, me, pl.ds(0, TILES)), own_sem.at[pp])

    half_transform(0)
    for idx in range(8):
        load(1, idx).start()
    pl.semaphore_wait(barrier, DEV - 1)
    send_groups(0, FIRST_GROUPS)
    copy_own(0).start()
    for pp in range(1, PAIRS):
        half_transform(pp)
        if pp < PAIRS - 1:
            for idx in range(8):
                load(pp + 1, idx).start()
        send_groups(pp, LATER_GROUPS)
        copy_own(pp).start()

    spread = dot(onehot(iota((K8, N), 0) // 8 == iota((K8, N), 1)), c, ((1,), (1,))).astype(jnp.bfloat16)
    col, p_row = iota((N, KP), 1), iota((N, KP), 0)
    same = iota((K8, KP), 0) % 8 == iota((K8, KP), 1) % 8
    for pp in range(PAIRS):
        full = dot(spread, onehot(p_row == (col // 16) * COLS + 2 * pp + (col % 16) // 8))
        kc = jnp.where(same, full, 0.0).astype(jnp.bfloat16)
        if pp < PAIRS - 1:
            kc_first[:, pp * KP:(pp + 1) * KP] = kc
        else:
            kc_ref[...] = kc

    for pp in range(PAIRS - 1):
        copy_own(pp).wait()

        @pl.loop(1, DEV)
        def _(k):
            wait_recv(pp, (me + k) % DEV)

    def rhs_first(tile):
        return jnp.concatenate([g_first[pp, :, tile].reshape(KP, 128) for pp in range(PAIRS - 1)], axis=0)

    for third, vm_ref in enumerate((vm0_ref, vm1_ref, vm2_ref)):
        @pl.loop(0, 4)
        def _(g):
            for n in range(2):
                rhs = jnp.concatenate([rhs_first((4 * third + g) * 4 + 2 * n + t) for t in range(2)], axis=1)
                vm_ref[g, :, n * 256:(n + 1) * 256] = dot(kc_first[...], rhs)

    @pl.loop(0, 6)
    def _(u):
        vh_ref[u] = dot(kc_first[...], rhs_first(48 + u))

    for pp in range(PAIRS):
        @pl.loop(1, DEV)
        def _(k):
            copy_out(pp, (me + k) % DEV).wait_send()

    copy_own(PAIRS - 1).wait()

    @pl.loop(1, DEV)
    def _(k):
        wait_recv(PAIRS - 1, (me + k) % DEV)


def last_kernel(g_ref, vm0_ref, vm1_ref, vm2_ref, vh_ref, kc_ref, v_ref):
    u = pl.program_id(0)
    kc = kc_ref[...]
    for third, vm_ref in enumerate((vm0_ref, vm1_ref, vm2_ref)):
        @pl.when(u // 2 == third)
        def _():
            for gg in range(2):
                g = 2 * u + gg
                for n in range(2):
                    rhs = jnp.concatenate([g_ref[:, g * 4 + 2 * n + t].reshape(KP, 128) for t in range(2)], axis=1)
                    out = vm_ref[g - 4 * third, :, n * 256:(n + 1) * 256] + dot(kc, rhs)
                    v_ref[:, gg * 8:(gg + 1) * 8, n * 256:(n + 1) * 256] = out.reshape(N, 8, 256)

    out = vh_ref[u] + dot(kc, g_ref[:, 48 + u].reshape(KP, 128))
    v_ref[:, 0:8, 512:576] = out.reshape(N, 8, 128)[:, :, :64]
    v_ref[:, 8:16, 512:576] = pltpu.roll(out, 64, 1).reshape(N, 8, 128)[:, :, :64]


def solution(mesh):
    def local_transform(ao_rows, coeffs):
        vmem = pl.BlockSpec(memory_space=pltpu.VMEM)
        hbm = pl.BlockSpec(memory_space=pltpu.HBM)
        parts = pl.pallas_call(
            exchange_kernel,
            out_shape=(pltpu.VMEM((DEV, TILES, 16, 128), jnp.bfloat16),
                       *[pltpu.VMEM((4, K8, 512), jnp.float32)] * 3,
                       pltpu.VMEM((6, K8, 128), jnp.float32),
                       pltpu.VMEM((K8, KP), jnp.bfloat16)),
            in_specs=[hbm, hbm],
            out_specs=(vmem,) * 6,
            scratch_shapes=[
                pltpu.VMEM((2, N, N, N), jnp.bfloat16),
                pltpu.VMEM((N, N), jnp.bfloat16),
                pltpu.VMEM((2, N * QPAD, 128), jnp.float32),
                pltpu.VMEM((PAIRS, DEV, TILES, 16, 128), jnp.bfloat16),
                pltpu.VMEM((PAIRS - 1, DEV, TILES, 16, 128), jnp.bfloat16),
                pltpu.VMEM((2 * N, 2 * N), jnp.bfloat16),
                pltpu.VMEM((K8, (PAIRS - 1) * KP), jnp.bfloat16),
                pltpu.SemaphoreType.DMA((8,)),
                pltpu.SemaphoreType.DMA,
                pltpu.SemaphoreType.DMA((PAIRS, DEV)),
                pltpu.SemaphoreType.DMA((PAIRS, DEV)),
                pltpu.SemaphoreType.DMA((PAIRS,)),
            ],
            compiler_params=pltpu.CompilerParams(collective_id=0, has_side_effects=True, vmem_limit_bytes=34 * 2**20),
            cost_estimate=pl.CostEstimate(flops=10**10, bytes_accessed=40 * 10**6, transcendentals=0),
            name='exchange',
        )(*[pltpu.with_memory_space_constraint(x, pltpu.HBM) for x in (ao_rows, coeffs)])
        return pl.pallas_call(
            last_kernel,
            grid=(6,),
            out_shape=jax.ShapeDtypeStruct((N, N, COLS * N), jnp.float32),
            in_specs=[vmem] * 6,
            out_specs=pl.BlockSpec((N, 16, COLS * N), lambda u: (0, u, 0)),
            compiler_params=pltpu.CompilerParams(vmem_limit_bytes=12 * 2**20),
            cost_estimate=pl.CostEstimate(flops=3 * 10**9, bytes_accessed=24 * 10**6, transcendentals=0),
            name='last_product',
        )(*[pltpu.with_memory_space_constraint(x, pltpu.VMEM) for x in parts])

    return jax.shard_map(local_transform, mesh=mesh, in_specs=(P(('frag', 'dev')), P('frag')), out_specs=P('frag', None, 'dev'), check_vma=False)
```

time: 262 us -> 252 us (0.962)
  Pallas kernels: 261 us -> 252 us
    pallas_call x1, Pallas kernels: 14.8 us -> 9.9 us  [local_transform(): pl.pallas_call(last_kernel, grid=(6,), out_shape=jax.ShapeDtypeStruct((N,...]
    pallas_call x1, Pallas kernels: 246 us -> 242 us  [local_transform(): pl.pallas_call(exchange_kernel, out_shape=(pltpu.VMEM((DEV, TILES, 16, 12...]
where the time goes in v5:
time: 252 us
  Pallas kernels  252 us (100%)
    pallas_call x1, Pallas kernels, local_transform(): pl.pallas_call(exchange_kernel, out_shape=(pltpu.VMEM((DEV, TILES, 16, 12...  242 us
    pallas_call x1, Pallas kernels, local_transform(): pl.pallas_call(last_kernel, grid=(6,), out_shape=jax.ShapeDtypeStruct((N,...  9.9 us

profile of v5, /device:TPU:1, one launch (start us, length us, event | category | flops | bytes accessed | tf_op | source)
XLA Modules:
  0.0 251.5 jit_solution(13793711549166509380)
XLA Ops:
  0.0 241.6 %exchange.1 = (bf16[16,54,16,128]{3,2,1,0:T(8,128)(2,1)S(1)}, f32[4,768,512]{2,1,0:T(8,128)S(1)}, f32[4,768,512]{2,1,0:T(8,128)S(1)}, f32[4,768,512]{2,1,0:T(8,1...) custom-call(bf16[6,96,96,96]{3,2,1,0:T(8,128)(2,1)} %a_hbm.1, bf16[96,96]{1,0:T(8,128)(2,1)} %c_hbm.1), custom_call_target="tpu_custom_call" | custom-call | flops 10000000000 | bytes 40000000 | tf_op jit(solution)/shard_map/exchange/pallas_call | solution.py:240
  241.6 9.9 %last_product.1 = f32[96,96,576]{2,1,0:T(8,128)} custom-call(bf16[16,54,16,128]{3,2,1,0:T(8,128)(2,1)S(1)} %get-tuple-element.11.g_ref, f32[4,768,512]{2,1,0:T(8,128)S(1)} %get-tuple-element.12.vm0_ref, f32[4,768,512]{2,1,0:T(8,128)S(1)} %get-tuple-element.13.vm1_ref, f32[4,768,512]{2,1,0:T(8,128)S(1)} %get-tuple-element.14.vm2_ref, ...), custom_call_target="tpu_custom_call" | custom-call | flops 3000000000 | bytes 24000000 | tf_op jit(solution)/shard_map/last_product/pallas_call | solution.py:266

commit v6 on v5

--- a/solution.py
+++ b/solution.py
@@ -16,8 +16,9 @@
 PART = 9
 K8 = 8 * N
 KP = 16 * DEV
-FIRST_GROUPS = ((7, 4), (6, 5), (3, 1), (2, 0))
-LATER_GROUPS = ((7, 4, 3, 1, 6, 5, 2, 0),)
+HEAD = 32
+FIRST_GROUPS = ((2, 3), (4, 5, 6, 7))
+LATER_GROUPS = ((0, 3, 4, 6, 1, 2, 5, 7),)
 
 
 def iota(shape, dim):
@@ -33,12 +34,16 @@
 
 
 def exchange_kernel(a_hbm, c_hbm, g_last, vm0_ref, vm1_ref, vm2_ref, vh_ref, kc_ref,
-                    a_vm, c_vm, h_scr, send, g_first, cc_ref, kc_first, a_sem, c_sem, send_sem, recv_sem, own_sem):
+                    a_vm, c_vm, ct_ref, h_scr, send, g_first, cc_ref, kc_first, a_sem, c_sem, send_sem, recv_sem, own_sem):
     frag = lax.axis_index('frag')
     me = lax.axis_index('dev')
     chip, core = me // 2, me % 2
     cz1, cz0, cy = chip // 4, (chip // 2) % 2, chip % 2
 
+    def chip_of(slot):
+        m = 7 - slot
+        return 4 * ((cz1 + m // 4) % 2) + 2 * ((cz0 + (m // 2) % 2) % 2) + (cy + m % 2) % 2
+
     def load(pp, idx):
         p2, quarter = idx // 4, pl.ds((idx % 4) * QB, QB)
         return pltpu.make_async_copy(a_hbm.at[2 * pp + p2, quarter], a_vm.at[p2, quarter], a_sem.at[idx])
@@ -56,8 +61,9 @@
 
     load_c.wait()
     c = c_vm[...]
-    eye = onehot(iota((N, N), 0) == iota((N, N), 1))
-    ct = dot(eye, c, ((1,), (1,))).astype(jnp.bfloat16)
+    j_row = iota((N, N), 0)
+    pick_j = onehot(iota((N, N), 1) == 2 * COLS * chip_of(j_row // (2 * COLS)) + j_row % (2 * COLS))
+    ct_ref[...] = dot(pick_j, c, ((1,), (1,))).astype(jnp.bfloat16)
     stacked = dot(onehot(iota((256, N), 0) % 128 == iota((256, N), 1)), c).astype(jnp.bfloat16)
     both = dot(stacked, onehot(iota((N, 256), 1) % 128 == iota((N, 256), 0)))
     c_two = jnp.where(iota((256, 256), 0) // 128 == iota((256, 256), 1) // 128, both, 0.0).astype(jnp.bfloat16)
@@ -71,9 +77,6 @@
 
     lane = iota((N, 128), 1)
 
-    def chip_at(m):
-        return 4 * ((cz1 + m // 4) % 2) + 2 * ((cz0 + (m // 2) % 2) % 2) + (cy + m % 2) % 2
-
     def block(pp, src, tiles):
         if isinstance(pp, int) and pp == PAIRS - 1:
             return g_last.at[src, tiles]
@@ -98,27 +101,30 @@
             device_id=(frag, src), device_id_type=MESH,
         ).wait_recv()
 
-    def half_transform(pp):
-        @pl.loop(0, 8)
-        def _(idx):
-            load(pp, idx).wait()
-            p2, q0 = idx // 4, (idx % 4) * QB
+    def half_transform(pp, first, rows, loads, wait=True):
+        @pl.loop(0, 8 // loads)
+        def _(step):
+            if wait:
+                for i in range(loads):
+                    load(pp, step * loads + i).wait()
+            p2, q0 = step * loads // 4, (step * loads % 4) * QB
             t_rows = []
-            for i in range(0, QB, 2):
+            for i in range(0, loads * QB, 2):
                 two = jnp.concatenate([a_vm[p2, q0 + i], gap, a_vm[p2, q0 + i + 1], gap], axis=1)
-                t_rows.append(dot(ct, two).astype(jnp.bfloat16))
+                t_rows.append(dot(ct_ref[first:first + rows], two).astype(jnp.bfloat16))
             half = dot(jnp.concatenate(t_rows, axis=0), c_two)
-            for i in range(QB):
-                rows = half[(i // 2) * N:(i // 2 + 1) * N, (i % 2) * 128:(i % 2 + 1) * 128]
-                h_scr[p2, pl.ds(q0 + i, N, stride=QPAD), :] = rows
-
-    def pack(pp, dest_chip):
+            for i in range(loads * QB):
+                part = half[(i // 2) * rows:(i // 2 + 1) * rows, (i % 2) * 128:(i % 2 + 1) * 128]
+                h_scr[p2, pl.ds(first * QPAD + q0 + i, rows, stride=QPAD), :] = part
+
+    def pack(pp, slot):
+        dest_chip = chip_of(slot)
         halves = []
         for p in range(2):
             tiles, last = [], []
             for cc in range(2):
-                j0 = (dest_chip * 2 + cc) * COLS
-                x = [h_scr[p, pl.ds(pl.multiple_of((j0 + l) * QPAD, 8), N), :] for l in range(COLS)]
+                j0 = (slot * 2 + cc) * COLS
+                x = [h_scr[p, pl.ds((j0 + l) * QPAD, N), :] for l in range(COLS)]
                 r1, r2, r3 = pltpu.roll(x[1], 96, 1), pltpu.roll(x[2], 64, 1), pltpu.roll(x[3], 32, 1)
                 r5 = pltpu.roll(x[5], 96, 1)
                 tiles += [jnp.where(lane < 96, x[0], r1), jnp.where(lane < 64, r1, r2),
@@ -142,29 +148,31 @@
 
     def send_groups(pp, groups):
         for group in groups:
-            for m in group:
-                pack(pp, chip_at(m))
+            for slot in group:
+                pack(pp, slot)
 
             @pl.loop(0, TILES // PART)
             def _(part):
                 for cc in range(2):
-                    for m in group:
-                        if m > 0:
-                            copy_out(pp, chip_at(m) * 2 + cc, part).start()
+                    for slot in group:
+                        if slot < 7:
+                            copy_out(pp, chip_of(slot) * 2 + cc, part).start()
                         elif cc == 1:
                             copy_out(pp, chip * 2 + 1 - core, part).start()
 
     def copy_own(pp):
         return pltpu.make_async_copy(send.at[pp, me], block(pp, me, pl.ds(0, TILES)), own_sem.at[pp])
 
-    half_transform(0)
+    half_transform(0, 0, HEAD, 2)
+    pl.semaphore_wait(barrier, DEV - 1)
+    send_groups(0, ((0, 1),))
+    half_transform(0, HEAD, N - HEAD, 1, wait=False)
     for idx in range(8):
         load(1, idx).start()
-    pl.semaphore_wait(barrier, DEV - 1)
     send_groups(0, FIRST_GROUPS)
     copy_own(0).start()
     for pp in range(1, PAIRS):
-        half_transform(pp)
+        half_transform(pp, 0, N, 1)
         if pp < PAIRS - 1:
             for idx in range(8):
                 load(pp + 1, idx).start()
@@ -216,21 +224,25 @@
 
 
 def last_kernel(g_ref, vm0_ref, vm1_ref, vm2_ref, vh_ref, kc_ref, v_ref):
-    u = pl.program_id(0)
+    g = pl.program_id(0)
     kc = kc_ref[...]
     for third, vm_ref in enumerate((vm0_ref, vm1_ref, vm2_ref)):
-        @pl.when(u // 2 == third)
+        @pl.when(g // 4 == third)
         def _():
-            for gg in range(2):
-                g = 2 * u + gg
-                for n in range(2):
-                    rhs = jnp.concatenate([g_ref[:, g * 4 + 2 * n + t].reshape(KP, 128) for t in range(2)], axis=1)
-                    out = vm_ref[g - 4 * third, :, n * 256:(n + 1) * 256] + dot(kc, rhs)
-                    v_ref[:, gg * 8:(gg + 1) * 8, n * 256:(n + 1) * 256] = out.reshape(N, 8, 256)
-
-    out = vh_ref[u] + dot(kc, g_ref[:, 48 + u].reshape(KP, 128))
-    v_ref[:, 0:8, 512:576] = out.reshape(N, 8, 128)[:, :, :64]
-    v_ref[:, 8:16, 512:576] = pltpu.roll(out, 64, 1).reshape(N, 8, 128)[:, :, :64]
+            for n in range(2):
+                rhs = jnp.concatenate([g_ref[:, g * 4 + 2 * n + t].reshape(KP, 128) for t in range(2)], axis=1)
+                out = vm_ref[g - 4 * third, :, n * 256:(n + 1) * 256] + dot(kc, rhs)
+                v_ref[:, :, n * 256:(n + 1) * 256] = out.reshape(N, 8, 256)
+
+    both = vh_ref[g // 2] + dot(kc, g_ref[:, 48 + g // 2].reshape(KP, 128))
+
+    @pl.when(g % 2 == 0)
+    def _():
+        v_ref[:, :, 512:576] = both.reshape(N, 8, 128)[:, :, :64]
+
+    @pl.when(g % 2 == 1)
+    def _():
+        v_ref[:, :, 512:576] = pltpu.roll(both, 64, 1).reshape(N, 8, 128)[:, :, :64]
 
 
 def solution(mesh):
@@ -247,6 +259,7 @@
             out_specs=(vmem,) * 6,
             scratch_shapes=[
                 pltpu.VMEM((2, N, N, N), jnp.bfloat16),
+                pltpu.VMEM((N, N), jnp.bfloat16),
                 pltpu.VMEM((N, N), jnp.bfloat16),
                 pltpu.VMEM((2, N * QPAD, 128), jnp.float32),
                 pltpu.VMEM((PAIRS, DEV, TILES, 16, 128), jnp.bfloat16),
@@ -265,10 +278,10 @@
         )(*[pltpu.with_memory_space_constraint(x, pltpu.HBM) for x in (ao_rows, coeffs)])
         return pl.pallas_call(
             last_kernel,
-            grid=(6,),
+            grid=(12,),
             out_shape=jax.ShapeDtypeStruct((N, N, COLS * N), jnp.float32),
             in_specs=[vmem] * 6,
-            out_specs=pl.BlockSpec((N, 16, COLS * N), lambda u: (0, u, 0)),
+            out_specs=pl.BlockSpec((N, 8, COLS * N), lambda g: (0, g, 0)),
             compiler_params=pltpu.CompilerParams(vmem_limit_bytes=12 * 2**20),
             cost_estimate=pl.CostEstimate(flops=3 * 10**9, bytes_accessed=24 * 10**6, transcendentals=0),
             name='last_product',

time: 252 us -> 252 us (level)
    pallas_call x1, Pallas kernels: 9.9 us -> 13.2 us  [local_transform(): pl.pallas_call(last_kernel, grid=(12,), out_shape=jax.ShapeDtypeStruct((N...]
    pallas_call x1, Pallas kernels: 242 us -> 239 us  [local_transform(): pl.pallas_call(exchange_kernel, out_shape=(pltpu.VMEM((DEV, TILES, 16, 12...]
where the time goes in v6:
time: 252 us
  Pallas kernels  252 us (100%)
    pallas_call x1, Pallas kernels, local_transform(): pl.pallas_call(exchange_kernel, out_shape=(pltpu.VMEM((DEV, TILES, 16, 12...  239 us
    pallas_call x1, Pallas kernels, local_transform(): pl.pallas_call(last_kernel, grid=(12,), out_shape=jax.ShapeDtypeStruct((N...  13.2 us

profile of v6, /device:TPU:1, one launch (start us, length us, event | category | flops | bytes accessed | tf_op | source)
XLA Modules:
  0.0 252.0 jit_solution(5183036145496950524)
XLA Ops:
  0.0 238.8 %exchange.1 = (bf16[16,54,16,128]{3,2,1,0:T(8,128)(2,1)S(1)}, f32[4,768,512]{2,1,0:T(8,128)S(1)}, f32[4,768,512]{2,1,0:T(8,128)S(1)}, f32[4,768,512]{2,1,0:T(8,1...) custom-call(bf16[6,96,96,96]{3,2,1,0:T(8,128)(2,1)} %a_hbm.1, bf16[96,96]{1,0:T(8,128)(2,1)} %c_hbm.1), custom_call_target="tpu_custom_call" | custom-call | flops 10000000000 | bytes 40000000 | tf_op jit(solution)/shard_map/exchange/pallas_call | solution.py:252
  238.8 13.2 %last_product.1 = f32[96,96,576]{2,1,0:T(8,128)} custom-call(bf16[16,54,16,128]{3,2,1,0:T(8,128)(2,1)S(1)} %get-tuple-element.11.g_ref, f32[4,768,512]{2,1,0:T(8,128)S(1)} %get-tuple-element.12.vm0_ref, f32[4,768,512]{2,1,0:T(8,128)S(1)} %get-tuple-element.13.vm1_ref, f32[4,768,512]{2,1,0:T(8,128)S(1)} %get-tuple-element.14.vm2_ref, ...), custom_call_target="tpu_custom_call" | custom-call | flops 3000000000 | bytes 24000000 | tf_op jit(solution)/shard_map/last_product/pallas_call | solution.py:279

commit v7 on v6

--- a/solution.py
+++ b/solution.py
@@ -223,26 +223,32 @@
         wait_recv(PAIRS - 1, (me + k) % DEV)
 
 
-def last_kernel(g_ref, vm0_ref, vm1_ref, vm2_ref, vh_ref, kc_ref, v_ref):
-    g = pl.program_id(0)
-    kc = kc_ref[...]
+def last_kernel(g_ref, vm0_ref, vm1_ref, vm2_ref, vh_ref, kc_ref, v_hbm, slots, sems):
+    def put(g, slot):
+        rows = pl.ds(pl.multiple_of(8 * g, 8), 8)
+        return pltpu.make_async_copy(slots.at[slot], v_hbm.at[:, rows], sems.at[slot])
+
     for third, vm_ref in enumerate((vm0_ref, vm1_ref, vm2_ref)):
-        @pl.when(g // 4 == third)
-        def _():
-            for n in range(2):
-                rhs = jnp.concatenate([g_ref[:, g * 4 + 2 * n + t].reshape(KP, 128) for t in range(2)], axis=1)
-                out = vm_ref[g - 4 * third, :, n * 256:(n + 1) * 256] + dot(kc, rhs)
-                v_ref[:, :, n * 256:(n + 1) * 256] = out.reshape(N, 8, 256)
-
-    both = vh_ref[g // 2] + dot(kc, g_ref[:, 48 + g // 2].reshape(KP, 128))
-
-    @pl.when(g % 2 == 0)
-    def _():
-        v_ref[:, :, 512:576] = both.reshape(N, 8, 128)[:, :, :64]
-
-    @pl.when(g % 2 == 1)
-    def _():
-        v_ref[:, :, 512:576] = pltpu.roll(both, 64, 1).reshape(N, 8, 128)[:, :, :64]
+        @pl.loop(0, 2)
+        def _(h):
+            u = 2 * third + h
+            kc = kc_ref[...]
+            both = vh_ref[u] + dot(kc, g_ref[:, 48 + u].reshape(KP, 128))
+            for parity in range(2):
+                slot = 2 * h + parity
+                g = 4 * third + slot
+                if third > 0:
+                    put(g - 4, slot).wait()
+                for n in range(2):
+                    rhs = jnp.concatenate([g_ref[:, g * 4 + 2 * n + t].reshape(KP, 128) for t in range(2)], axis=1)
+                    out = vm_ref[slot, :, n * 256:(n + 1) * 256] + dot(kc, rhs)
+                    slots[slot, :, :, n * 256:(n + 1) * 256] = out.reshape(N, 8, 256)
+                edge = both if parity == 0 else pltpu.roll(both, 64, 1)
+                slots[slot, :, :, 512:576] = edge.reshape(N, 8, 128)[:, :, :64]
+                put(g, slot).start()
+
+    for slot in range(4):
+        put(8 + slot, slot).wait()
 
 
 def solution(mesh):
@@ -278,10 +284,10 @@
         )(*[pltpu.with_memory_space_constraint(x, pltpu.HBM) for x in (ao_rows, coeffs)])
         return pl.pallas_call(
             last_kernel,
-            grid=(12,),
             out_shape=jax.ShapeDtypeStruct((N, N, COLS * N), jnp.float32),
             in_specs=[vmem] * 6,
-            out_specs=pl.BlockSpec((N, 8, COLS * N), lambda g: (0, g, 0)),
+            out_specs=pl.BlockSpec(memory_space=pltpu.HBM),
+            scratch_shapes=[pltpu.VMEM((4, N, 8, COLS * N), jnp.float32), pltpu.SemaphoreType.DMA((4,))],
             compiler_params=pltpu.CompilerParams(vmem_limit_bytes=12 * 2**20),
             cost_estimate=pl.CostEstimate(flops=3 * 10**9, bytes_accessed=24 * 10**6, transcendentals=0),
             name='last_product',

time: 252 us -> 247 us (0.980)
  Pallas kernels: 252 us -> 247 us
    pallas_call x1, Pallas kernels: 13.2 us -> 8.45 us  [local_transform(): pl.pallas_call(last_kernel, out_shape=jax.ShapeDtypeStruct((N, N, COLS *...]
where the time goes in v7:
time: 247 us
  Pallas kernels  247 us (100%)
    pallas_call x1, Pallas kernels, local_transform(): pl.pallas_call(exchange_kernel, out_shape=(pltpu.VMEM((DEV, TILES, 16, 12...  239 us
    pallas_call x1, Pallas kernels, local_transform(): pl.pallas_call(last_kernel, out_shape=jax.ShapeDtypeStruct((N, N, COLS *...  8.45 us

profile of v7, /device:TPU:1, one launch (start us, length us, event | category | flops | bytes accessed | tf_op | source)
XLA Modules:
  0.0 247.2 jit_solution(7339273056756565825)
XLA Ops:
  0.0 238.8 %exchange.1 = (bf16[16,54,16,128]{3,2,1,0:T(8,128)(2,1)S(1)}, f32[4,768,512]{2,1,0:T(8,128)S(1)}, f32[4,768,512]{2,1,0:T(8,128)S(1)}, f32[4,768,512]{2,1,0:T(8,1...) custom-call(bf16[6,96,96,96]{3,2,1,0:T(8,128)(2,1)} %a_hbm.1, bf16[96,96]{1,0:T(8,128)(2,1)} %c_hbm.1), custom_call_target="tpu_custom_call" | custom-call | flops 10000000000 | bytes 40000000 | tf_op jit(solution)/shard_map/exchange/pallas_call | solution.py:258
  238.8 8.4 %last_product.1 = f32[96,96,576]{2,1,0:T(8,128)} custom-call(bf16[16,54,16,128]{3,2,1,0:T(8,128)(2,1)S(1)} %get-tuple-element.11.g_ref, f32[4,768,512]{2,1,0:T(8,128)S(1)} %get-tuple-element.12.vm0_ref, f32[4,768,512]{2,1,0:T(8,128)S(1)} %get-tuple-element.13.vm1_ref, f32[4,768,512]{2,1,0:T(8,128)S(1)} %get-tuple-element.14.vm2_ref, ...), custom_call_target="tpu_custom_call" | custom-call | flops 3000000000 | bytes 24000000 | tf_op jit(solution)/shard_map/last_product/pallas_call | solution.py:285

commit v8 on v7

--- a/solution.py
+++ b/solution.py
@@ -16,8 +16,8 @@
 PART = 9
 K8 = 8 * N
 KP = 16 * DEV
-HEAD = 32
-FIRST_GROUPS = ((2, 3), (4, 5, 6, 7))
+HEAD = 16
+FIRST_GROUPS = ((1, 2, 3), (4, 5, 6, 7))
 LATER_GROUPS = ((0, 3, 4, 6, 1, 2, 5, 7),)
 
 
@@ -68,13 +68,6 @@
     both = dot(stacked, onehot(iota((N, 256), 1) % 128 == iota((N, 256), 0)))
     c_two = jnp.where(iota((256, 256), 0) // 128 == iota((256, 256), 1) // 128, both, 0.0).astype(jnp.bfloat16)
     gap = jnp.zeros((N, 32), jnp.bfloat16)
-    row = iota((2 * N, N), 0)
-    pick_a = onehot(iota((2 * N, N), 1) == 8 * (row // 16) + row % 8)
-    c_rows = dot(pick_a, c, ((1,), (1,))).astype(jnp.bfloat16)
-    wide = dot(c_rows, onehot(iota((N, 2 * N), 1) % N == iota((N, 2 * N), 0)))
-    same_p = (iota((2 * N, 2 * N), 0) % 16) // 8 == iota((2 * N, 2 * N), 1) // N
-    cc_ref[...] = jnp.where(same_p, wide, 0.0).astype(jnp.bfloat16)
-
     lane = iota((N, 128), 1)
 
     def block(pp, src, tiles):
@@ -153,19 +146,25 @@
 
             @pl.loop(0, TILES // PART)
             def _(part):
-                for cc in range(2):
-                    for slot in group:
+                for turn in range(2):
+                    for n, slot in enumerate(group):
                         if slot < 7:
-                            copy_out(pp, chip_of(slot) * 2 + cc, part).start()
-                        elif cc == 1:
+                            copy_out(pp, chip_of(slot) * 2 + (core + turn + n) % 2, part).start()
+                        elif turn == 1:
                             copy_out(pp, chip * 2 + 1 - core, part).start()
 
     def copy_own(pp):
         return pltpu.make_async_copy(send.at[pp, me], block(pp, me, pl.ds(0, TILES)), own_sem.at[pp])
 
     half_transform(0, 0, HEAD, 2)
+    row = iota((2 * N, N), 0)
+    pick_a = onehot(iota((2 * N, N), 1) == 8 * (row // 16) + row % 8)
+    c_rows = dot(pick_a, c, ((1,), (1,))).astype(jnp.bfloat16)
+    wide = dot(c_rows, onehot(iota((N, 2 * N), 1) % N == iota((N, 2 * N), 0)))
+    same_p = (iota((2 * N, 2 * N), 0) % 16) // 8 == iota((2 * N, 2 * N), 1) // N
+    cc_ref[...] = jnp.where(same_p, wide, 0.0).astype(jnp.bfloat16)
     pl.semaphore_wait(barrier, DEV - 1)
-    send_groups(0, ((0, 1),))
+    send_groups(0, ((0,),))
     half_transform(0, HEAD, N - HEAD, 1, wait=False)
     for idx in range(8):
         load(1, idx).start()

time: 247 us -> 252 us (1.020)
  Pallas kernels: 247 us -> 251 us
    pallas_call x1, Pallas kernels: 239 us -> 242 us  [local_transform(): pl.pallas_call(exchange_kernel, out_shape=(pltpu.VMEM((DEV, TILES, 16, 12...]
where the time goes in v8:
time: 252 us; the launch traced here: 251 us
  Pallas kernels  251 us (100%)
    pallas_call x1, Pallas kernels, local_transform(): pl.pallas_call(exchange_kernel, out_shape=(pltpu.VMEM((DEV, TILES, 16, 12...  242 us
    pallas_call x1, Pallas kernels, local_transform(): pl.pallas_call(last_kernel, out_shape=jax.ShapeDtypeStruct((N, N, COLS *...  8.45 us

profile of v8, /device:TPU:1, one launch (start us, length us, event | category | flops | bytes accessed | tf_op | source)
XLA Modules:
  0.0 250.8 jit_solution(10545706137921222551)
XLA Ops:
  0.0 242.4 %exchange.1 = (bf16[16,54,16,128]{3,2,1,0:T(8,128)(2,1)S(1)}, f32[4,768,512]{2,1,0:T(8,128)S(1)}, f32[4,768,512]{2,1,0:T(8,128)S(1)}, f32[4,768,512]{2,1,0:T(8,1...) custom-call(bf16[6,96,96,96]{3,2,1,0:T(8,128)(2,1)} %a_hbm.1, bf16[96,96]{1,0:T(8,128)(2,1)} %c_hbm.1), custom_call_target="tpu_custom_call" | custom-call | flops 10000000000 | bytes 40000000 | tf_op jit(solution)/shard_map/exchange/pallas_call | solution.py:257
  242.4 8.4 %last_product.1 = f32[96,96,576]{2,1,0:T(8,128)} custom-call(bf16[16,54,16,128]{3,2,1,0:T(8,128)(2,1)S(1)} %get-tuple-element.11.g_ref, f32[4,768,512]{2,1,0:T(8,128)S(1)} %get-tuple-element.12.vm0_ref, f32[4,768,512]{2,1,0:T(8,128)S(1)} %get-tuple-element.13.vm1_ref, f32[4,768,512]{2,1,0:T(8,128)S(1)} %get-tuple-element.14.vm2_ref, ...), custom_call_target="tpu_custom_call" | custom-call | flops 3000000000 | bytes 24000000 | tf_op jit(solution)/shard_map/last_product/pallas_call | solution.py:284

commit v9 on v8

--- a/solution.py
+++ b/solution.py
@@ -17,7 +17,7 @@
 K8 = 8 * N
 KP = 16 * DEV
 HEAD = 16
-FIRST_GROUPS = ((1, 2, 3), (4, 5, 6, 7))
+FIRST_GROUPS = ((3, 4, 6, 1, 2, 5, 7),)
 LATER_GROUPS = ((0, 3, 4, 6, 1, 2, 5, 7),)
 
 
@@ -147,9 +147,9 @@
             @pl.loop(0, TILES // PART)
             def _(part):
                 for turn in range(2):
-                    for n, slot in enumerate(group):
+                    for slot in group:
                         if slot < 7:
-                            copy_out(pp, chip_of(slot) * 2 + (core + turn + n) % 2, part).start()
+                            copy_out(pp, chip_of(slot) * 2 + turn, part).start()
                         elif turn == 1:
                             copy_out(pp, chip * 2 + 1 - core, part).start()
 

time: 252 us -> 250 us (level)
  no operation moved by 1% of the time
where the time goes in v9:
time: 250 us
  Pallas kernels  250 us (100%)
    pallas_call x1, Pallas kernels, local_transform(): pl.pallas_call(exchange_kernel, out_shape=(pltpu.VMEM((DEV, TILES, 16, 12...  241 us
    pallas_call x1, Pallas kernels, local_transform(): pl.pallas_call(last_kernel, out_shape=jax.ShapeDtypeStruct((N, N, COLS *...  8.45 us

profile of v9, /device:TPU:1, one launch (start us, length us, event | category | flops | bytes accessed | tf_op | source)
XLA Modules:
  0.0 249.9 jit_solution(3523722287883580954)
XLA Ops:
  0.0 241.4 %exchange.1 = (bf16[16,54,16,128]{3,2,1,0:T(8,128)(2,1)S(1)}, f32[4,768,512]{2,1,0:T(8,128)S(1)}, f32[4,768,512]{2,1,0:T(8,128)S(1)}, f32[4,768,512]{2,1,0:T(8,1...) custom-call(bf16[6,96,96,96]{3,2,1,0:T(8,128)(2,1)} %a_hbm.1, bf16[96,96]{1,0:T(8,128)(2,1)} %c_hbm.1), custom_call_target="tpu_custom_call" | custom-call | flops 10000000000 | bytes 40000000 | tf_op jit(solution)/shard_map/exchange/pallas_call | solution.py:257
  241.4 8.4 %last_product.1 = f32[96,96,576]{2,1,0:T(8,128)} custom-call(bf16[16,54,16,128]{3,2,1,0:T(8,128)(2,1)S(1)} %get-tuple-element.11.g_ref, f32[4,768,512]{2,1,0:T(8,128)S(1)} %get-tuple-element.12.vm0_ref, f32[4,768,512]{2,1,0:T(8,128)S(1)} %get-tuple-element.13.vm1_ref, f32[4,768,512]{2,1,0:T(8,128)S(1)} %get-tuple-element.14.vm2_ref, ...), custom_call_target="tpu_custom_call" | custom-call | flops 3000000000 | bytes 24000000 | tf_op jit(solution)/shard_map/last_product/pallas_call | solution.py:284

commit v10 on v9

--- a/solution.py
+++ b/solution.py
@@ -13,11 +13,11 @@
 QPAD = 104
 QB = 24
 TILES = 54
-PART = 9
+PARTS = (9, 3, 3)
 K8 = 8 * N
 KP = 16 * DEV
-HEAD = 16
-FIRST_GROUPS = ((3, 4, 6, 1, 2, 5, 7),)
+HEAD = 32
+FIRST_GROUPS = ((2, 3), (4, 5, 6, 7))
 LATER_GROUPS = ((0, 3, 4, 6, 1, 2, 5, 7),)
 
 
@@ -76,7 +76,7 @@
         return g_first.at[pp, src, tiles]
 
     def copy_out(pp, dest, part=None):
-        tiles = pl.ds(0, TILES) if part is None else pl.ds(part * PART, PART)
+        tiles = pl.ds(0, TILES) if part is None else pl.ds(part * PARTS[pp], PARTS[pp])
         return pltpu.make_async_remote_copy(
             src_ref=send.at[pp, dest, tiles],
             dst_ref=block(pp, me, tiles),
@@ -144,13 +144,13 @@
             for slot in group:
                 pack(pp, slot)
 
-            @pl.loop(0, TILES // PART)
+            @pl.loop(0, TILES // PARTS[pp])
             def _(part):
-                for turn in range(2):
+                for cc in range(2):
                     for slot in group:
                         if slot < 7:
-                            copy_out(pp, chip_of(slot) * 2 + turn, part).start()
-                        elif turn == 1:
+                            copy_out(pp, chip_of(slot) * 2 + cc, part).start()
+                        elif cc == 1:
                             copy_out(pp, chip * 2 + 1 - core, part).start()
 
     def copy_own(pp):
@@ -164,7 +164,7 @@
     same_p = (iota((2 * N, 2 * N), 0) % 16) // 8 == iota((2 * N, 2 * N), 1) // N
     cc_ref[...] = jnp.where(same_p, wide, 0.0).astype(jnp.bfloat16)
     pl.semaphore_wait(barrier, DEV - 1)
-    send_groups(0, ((0,),))
+    send_groups(0, ((0, 1),))
     half_transform(0, HEAD, N - HEAD, 1, wait=False)
     for idx in range(8):
         load(1, idx).start()

time: 250 us -> 276 us (1.10)
  Pallas kernels: 250 us -> 275 us
    pallas_call x1, Pallas kernels: 241 us -> 267 us  [local_transform(): pl.pallas_call(exchange_kernel, out_shape=(pltpu.VMEM((DEV, TILES, 16, 12...]
where the time goes in v10:
time: 276 us; the launch traced here: 275 us
  Pallas kernels  275 us (100%)
    pallas_call x1, Pallas kernels, local_transform(): pl.pallas_call(exchange_kernel, out_shape=(pltpu.VMEM((DEV, TILES, 16, 12...  267 us
    pallas_call x1, Pallas kernels, local_transform(): pl.pallas_call(last_kernel, out_shape=jax.ShapeDtypeStruct((N, N, COLS *...  8.45 us

profile of v10, /device:TPU:1, one launch (start us, length us, event | category | flops | bytes accessed | tf_op | source)
XLA Modules:
  0.0 275.3 jit_solution(10470617855445896024)
XLA Ops:
  0.0 266.8 %exchange.1 = (bf16[16,54,16,128]{3,2,1,0:T(8,128)(2,1)S(1)}, f32[4,768,512]{2,1,0:T(8,128)S(1)}, f32[4,768,512]{2,1,0:T(8,128)S(1)}, f32[4,768,512]{2,1,0:T(8,1...) custom-call(bf16[6,96,96,96]{3,2,1,0:T(8,128)(2,1)} %a_hbm.1, bf16[96,96]{1,0:T(8,128)(2,1)} %c_hbm.1), custom_call_target="tpu_custom_call" | custom-call | flops 10000000000 | bytes 40000000 | tf_op jit(solution)/shard_map/exchange/pallas_call | solution.py:257
  266.8 8.5 %last_product.1 = f32[96,96,576]{2,1,0:T(8,128)} custom-call(bf16[16,54,16,128]{3,2,1,0:T(8,128)(2,1)S(1)} %get-tuple-element.11.g_ref, f32[4,768,512]{2,1,0:T(8,128)S(1)} %get-tuple-element.12.vm0_ref, f32[4,768,512]{2,1,0:T(8,128)S(1)} %get-tuple-element.13.vm1_ref, f32[4,768,512]{2,1,0:T(8,128)S(1)} %get-tuple-element.14.vm2_ref, ...), custom_call_target="tpu_custom_call" | custom-call | flops 3000000000 | bytes 24000000 | tf_op jit(solution)/shard_map/last_product/pallas_call | solution.py:284

commit v11 on v10

--- a/solution.py
+++ b/solution.py
@@ -13,7 +13,7 @@
 QPAD = 104
 QB = 24
 TILES = 54
-PARTS = (9, 3, 3)
+PARTS = (18, 18, 9)
 K8 = 8 * N
 KP = 16 * DEV
 HEAD = 32

time: 276 us -> 248 us (0.90)
  Pallas kernels: 275 us -> 248 us
    pallas_call x1, Pallas kernels: 267 us -> 239 us  [local_transform(): pl.pallas_call(exchange_kernel, out_shape=(pltpu.VMEM((DEV, TILES, 16, 12...]
where the time goes in v11:
time: 248 us
  Pallas kernels  248 us (100%)
    pallas_call x1, Pallas kernels, local_transform(): pl.pallas_call(exchange_kernel, out_shape=(pltpu.VMEM((DEV, TILES, 16, 12...  239 us
    pallas_call x1, Pallas kernels, local_transform(): pl.pallas_call(last_kernel, out_shape=jax.ShapeDtypeStruct((N, N, COLS *...  8.45 us

profile of v11, /device:TPU:1, one launch (start us, length us, event | category | flops | bytes accessed | tf_op | source)
XLA Modules:
  0.0 247.7 jit_solution(4971168718699981577)
XLA Ops:
  0.0 239.3 %exchange.1 = (bf16[16,54,16,128]{3,2,1,0:T(8,128)(2,1)S(1)}, f32[4,768,512]{2,1,0:T(8,128)S(1)}, f32[4,768,512]{2,1,0:T(8,128)S(1)}, f32[4,768,512]{2,1,0:T(8,1...) custom-call(bf16[6,96,96,96]{3,2,1,0:T(8,128)(2,1)} %a_hbm.1, bf16[96,96]{1,0:T(8,128)(2,1)} %c_hbm.1), custom_call_target="tpu_custom_call" | custom-call | flops 10000000000 | bytes 40000000 | tf_op jit(solution)/shard_map/exchange/pallas_call | solution.py:257
  239.3 8.5 %last_product.1 = f32[96,96,576]{2,1,0:T(8,128)} custom-call(bf16[16,54,16,128]{3,2,1,0:T(8,128)(2,1)S(1)} %get-tuple-element.11.g_ref, f32[4,768,512]{2,1,0:T(8,128)S(1)} %get-tuple-element.12.vm0_ref, f32[4,768,512]{2,1,0:T(8,128)S(1)} %get-tuple-element.13.vm1_ref, f32[4,768,512]{2,1,0:T(8,128)S(1)} %get-tuple-element.14.vm2_ref, ...), custom_call_target="tpu_custom_call" | custom-call | flops 3000000000 | bytes 24000000 | tf_op jit(solution)/shard_map/last_product/pallas_call | solution.py:284

commit v12 on v7

--- a/solution.py
+++ b/solution.py
@@ -176,7 +176,7 @@
         if pp < PAIRS - 1:
             for idx in range(8):
                 load(pp + 1, idx).start()
-        send_groups(pp, LATER_GROUPS)
+        send_groups(pp, ((0, 1, 2, 3), (4, 5, 6, 7)) if pp == 1 else LATER_GROUPS)
         copy_own(pp).start()
 
     spread = dot(onehot(iota((K8, N), 0) // 8 == iota((K8, N), 1)), c, ((1,), (1,))).astype(jnp.bfloat16)

time: 247 us -> 247 us (level)
  no operation moved by 1% of the time
where the time goes in v12:
time: 247 us
  Pallas kernels  247 us (100%)
    pallas_call x1, Pallas kernels, local_transform(): pl.pallas_call(exchange_kernel, out_shape=(pltpu.VMEM((DEV, TILES, 16, 12...  239 us
    pallas_call x1, Pallas kernels, local_transform(): pl.pallas_call(last_kernel, out_shape=jax.ShapeDtypeStruct((N, N, COLS *...  8.45 us

profile of v12, /device:TPU:1, one launch (start us, length us, event | category | flops | bytes accessed | tf_op | source)
XLA Modules:
  0.0 247.2 jit_solution(10167461908680294046)
XLA Ops:
  0.0 238.7 %exchange.1 = (bf16[16,54,16,128]{3,2,1,0:T(8,128)(2,1)S(1)}, f32[4,768,512]{2,1,0:T(8,128)S(1)}, f32[4,768,512]{2,1,0:T(8,128)S(1)}, f32[4,768,512]{2,1,0:T(8,1...) custom-call(bf16[6,96,96,96]{3,2,1,0:T(8,128)(2,1)} %a_hbm.1, bf16[96,96]{1,0:T(8,128)(2,1)} %c_hbm.1), custom_call_target="tpu_custom_call" | custom-call | flops 10000000000 | bytes 40000000 | tf_op jit(solution)/shard_map/exchange/pallas_call | solution.py:258
  238.7 8.4 %last_product.1 = f32[96,96,576]{2,1,0:T(8,128)} custom-call(bf16[16,54,16,128]{3,2,1,0:T(8,128)(2,1)S(1)} %get-tuple-element.11.g_ref, f32[4,768,512]{2,1,0:T(8,128)S(1)} %get-tuple-element.12.vm0_ref, f32[4,768,512]{2,1,0:T(8,128)S(1)} %get-tuple-element.13.vm1_ref, f32[4,768,512]{2,1,0:T(8,128)S(1)} %get-tuple-element.14.vm2_ref, ...), custom_call_target="tpu_custom_call" | custom-call | flops 3000000000 | bytes 24000000 | tf_op jit(solution)/shard_map/last_product/pallas_call | solution.py:285
